TPU v7x, 32 devices: a whole 2x2x4 slice. The times are simulated.
32 devices in a mesh: dp: 4 (over z), tensor: 8 (over y, x, core).
Axes of the slice: x: 2, y: 2, z: 4, core: 2. Of those that a mesh axis runs over, the one named last changes fastest.
Arguments:
- tokens: bfloat16 [1024, 4096], P(('dp', 'tensor')), may hold values from -4 to 4
- lengths: int32 [4], replicated, may hold values from 64 to 256, as said below
- norm_gains: float32 [2, 4096], replicated, may hold values from 0.25 to 1.75
- query_weight: bfloat16 [2, 4096, 4096], P(None, None, 'tensor'), may hold values from -0.09375 to 0.09375
- key_weight: bfloat16 [2, 4096, 1024], P(None, None, 'tensor'), may hold values from -0.09375 to 0.09375
- value_weight: bfloat16 [2, 4096, 1024], P(None, None, 'tensor'), may hold values from -0.09375 to 0.09375
- out_weight: bfloat16 [2, 4096, 4096], P(None, 'tensor'), may hold values from -0.09375 to 0.09375
- query_probe: bfloat16 [2, 4096, 4096], P(None, 'dp', 'tensor'), may hold values from -0.09375 to 0.09375
- key_probe: bfloat16 [2, 4096, 1024], P(None, 'dp', 'tensor'), may hold values from -0.09375 to 0.09375
- value_probe: bfloat16 [2, 4096, 1024], P(None, 'dp', 'tensor'), may hold values from -0.09375 to 0.09375
- out_probe: bfloat16 [2, 4096, 4096], P(None, 'tensor', 'dp'), may hold values from -0.09375 to 0.09375
Outputs:
- query_product: float32 [2, 4096, 4096], P(None, 'dp', 'tensor')
- key_product: float32 [2, 4096, 1024], P(None, 'dp', 'tensor')
- value_product: float32 [2, 4096, 1024], P(None, 'dp', 'tensor')
- out_product: float32 [2, 4096, 4096], P(None, 'tensor', 'dp')
Inputs may be any that keep to these rules, and one draw needn't show every extreme that they name: lengths[i] counts the leading valid positions of sequence i; the last sequence is full.
All inputs are finite; a program needn't handle non-finite values.
Results may differ from a plain program's by a relative error of at most 0.035.
Values may be sent and summed in bfloat16 or wider, within the bound.
A program may use at most 128 MiB of HBM per device.

v0:
```python
import functools
import math
import types

import jax
import jax.numpy as jnp
from jax import lax
from jax.experimental import pallas as pl
from jax.experimental.pallas import tpu as pltpu
from jax.sharding import PartitionSpec as P

HD = 128
LEN = 256
EPS = 1e-05
THETA = 500000.0
MESH = pl.DeviceIdType.MESH
SCALE = 1.0 / math.sqrt(HD)


def low(values):
    return values.astype(jnp.bfloat16)


def wide(values):
    return values.astype(jnp.float32)


def matmul(left_side, right_side):
    return jnp.dot(left_side, right_side, preferred_element_type=jnp.float32)


def contract_rows(left_side, right_side):
    return lax.dot_general(
        left_side, right_side, (((0,), (0,)), ((), ())), preferred_element_type=jnp.float32
    )


def contract_last(left_side, right_side):
    return lax.dot_general(
        left_side, right_side, (((1,), (1,)), ((), ())), preferred_element_type=jnp.float32
    )


def rope_tables(length, head_size):
    position = jnp.arange(length).astype(jnp.float32)
    column = jnp.arange(head_size // 2).astype(jnp.float32)
    frequency = jnp.exp(-math.log(THETA) * 2.0 * column / head_size)
    angles = position[:, None] * frequency[None, :]
    cosine, sine = jnp.cos(angles), jnp.sin(angles)
    return (
        jnp.concatenate([cosine, cosine], axis=-1),
        jnp.concatenate([-sine, sine], axis=-1),
    )


def flip(index, mask):
    result = index
    bit = 1
    while bit <= mask:
        if mask & bit:
            result = result + bit - 2 * bit * lax.rem(lax.div(index, bit), 2)
        bit *= 2
    return result


def semaphore_count(sizes):
    batches, width = sizes
    return 14 * width + 18 * batches


class Fabric:
    def __init__(self, sizes, send, recv):
        self.batches, self.width = sizes
        self.chips = self.width // 2
        self.row = lax.axis_index("dp")
        self.col = lax.axis_index("tensor")
        self.send, self.recv, self.used = send, recv, 0
        self.pending = []
        self.guarded = []

    def copy(self, source, target, row, col):
        number = self.used
        self.used += 1
        assert number < semaphore_count((self.batches, self.width))
        made = pltpu.make_async_remote_copy(
            src_ref=source,
            dst_ref=target,
            send_sem=self.send.at[number],
            recv_sem=self.recv.at[number],
            device_id=(row, col),
            device_id_type=MESH,
        )
        made.start()
        self.pending.append(made)
        return made

    def drain(self):
        for made in self.pending:
            made.wait_send()
        self.pending = []

    def drain_chains(self):
        for condition, made in self.guarded:
            pl.when(condition)(made.wait_send)
        self.guarded = []

    def mate(self):
        return flip(self.col, 1)

    def peer(self, step):
        return flip(self.col, 2 * step)

    def batch(self, step):
        return flip(self.row, step)

    def greet(self, along_tensor=True):
        barrier = pltpu.get_barrier_semaphore()
        peers = [(self.batch(step), self.col) for step in range(1, self.batches)]
        if along_tensor:
            peers += [(self.row, self.peer(step)) for step in range(1, self.chips)]
            peers.append((self.row, self.mate()))
        for peer in peers:
            pl.semaphore_signal(barrier, inc=1, device_id=peer, device_id_type=MESH)
        return lambda: pl.semaphore_wait(barrier, len(peers))

    def gather(self, source, slot):
        there = slot(self.col)
        direct = [
            self.copy(source, there, self.row, self.peer(step)) for step in range(1, self.chips)
        ]
        beside = [self.copy(source, there, self.row, self.mate())]
        there[...] = source[...]

        def forward():
            for step in range(1, self.chips):
                direct[step - 1].wait_recv()
                piece = slot(self.peer(step))
                beside.append(self.copy(piece, piece, self.row, self.mate()))

        def finish():
            for made in beside:
                made.wait_recv()

        return forward, finish

    def pair_up(self, slot, beside):
        return [
            self.copy(slot(flip(self.mate(), 2 * step)), beside.at[step], self.row, self.mate())
            for step in range(self.chips)
        ]

    def spread(self, slot, copies, beside, landed):
        def send(step):
            return self.copy(slot(self.peer(step)), landed.at[step], self.row, self.peer(step))

        sent = []
        order = list(range(self.chips - 1, 0, -1))
        for place, step in enumerate(order):
            copies[step].wait_recv()
            own = slot(self.peer(step))
            own[...] = low(wide(own[...]) + wide(beside[step]))
            if place:
                sent.append(send(order[place - 1]))
        copies[0].wait_recv()
        total = wide(slot(self.col)[...]) + wide(beside[0])
        if order:
            sent.append(send(order[-1]))

        def finish():
            result = total
            for made, step in zip(sent, order):
                made.wait_recv()
                result = result + wide(landed[step])
            return result

        return finish

    def exchange(self, source, target):
        made = [
            self.copy(
                source.at[self.batch(step)], target.at[self.row], self.batch(step), self.col
            )
            for step in range(1, self.batches)
        ]
        target[self.row] = source[self.row]

        def finish():
            for copy in made:
                copy.wait_recv()

        return finish

    def reserve(self, count):
        first = self.used
        self.used += count
        assert self.used <= semaphore_count((self.batches, self.width))
        return first

    def hop(self, source, target, number, way):
        return pltpu.make_async_remote_copy(
            src_ref=source,
            dst_ref=target,
            send_sem=self.send.at[number],
            recv_sem=self.recv.at[number],
            device_id=(jnp.clip(self.row + way, 0, self.batches - 1), self.col),
            device_id_type=MESH,
        )

    def rank(self, way):
        return self.row if way > 0 else self.batches - 1 - self.row


class GatherChain:
    def __init__(self, fabric, source, target):
        self.fabric, self.source, self.target = fabric, source, target
        self.first = fabric.reserve(2 * (fabric.batches - 1))

    def number(self, way, step):
        return self.first + (0 if way > 0 else self.fabric.batches - 1) + step - 1

    def arrive(self, step):
        fabric = self.fabric
        for way in (1, -1):
            piece = jnp.clip(fabric.row - way * step, 0, fabric.batches - 1)
            made = fabric.hop(
                self.target.at[piece], self.target.at[piece], self.number(way, step), way
            )
            pl.when(fabric.rank(way) >= step)(made.wait_recv)

    def step(self, step):
        fabric = self.fabric
        if step > 1:
            self.arrive(step - 1)
        for way in (1, -1):
            piece = jnp.clip(fabric.row - way * (step - 1), 0, fabric.batches - 1)
            source = self.source if step == 1 else self.target.at[piece]
            made = fabric.hop(source, self.target.at[piece], self.number(way, step), way)
            rank = fabric.rank(way)
            condition = (rank >= step - 1) & (rank < fabric.batches - 1)
            pl.when(condition)(made.start)
            fabric.guarded.append((condition, made))
        if step == 1:
            self.target[fabric.row] = self.source[...]

    def finish(self):
        self.arrive(self.fabric.batches - 1)


class ScatterChain:
    def __init__(self, fabric, source, landed):
        self.fabric, self.source, self.landed = fabric, source, landed
        self.first = fabric.reserve(2 * (fabric.batches - 1))

    def hop(self, source, way, step):
        side = 0 if way > 0 else 1
        number = self.first + side * (self.fabric.batches - 1) + step - 1
        return self.fabric.hop(source, self.landed.at[side, step - 1], number, way)

    def step(self, step):
        fabric = self.fabric
        last = fabric.batches - 1
        for way in (1, -1):
            side = 0 if way > 0 else 1
            rank = fabric.rank(way)
            goal = jnp.clip(fabric.batches + rank - step, 0, last)
            goal = goal if way > 0 else last - goal
            own = self.hop(self.source.at[goal], way, step)
            pl.when(rank == 0)(own.start)
            fabric.guarded.append((rank == 0, own))
            if step > 1:
                buffer = self.source.at[goal]
                summed = self.hop(buffer, way, step)
                before = self.hop(buffer, way, step - 1)
                condition = (rank > 0) & (rank < step)

                @pl.when(condition)
                def _():
                    before.wait_recv()
                    buffer[...] = low(wide(buffer[...]) + wide(self.landed[side, step - 2]))
                    summed.start()

                fabric.guarded.append((condition, summed))

    def finish(self, total):
        fabric = self.fabric
        last = fabric.batches - 1
        total[...] = wide(self.source[fabric.row])
        for way in (1, -1):
            side = 0 if way > 0 else 1
            made = self.hop(self.source.at[fabric.row], way, last)

            @pl.when(fabric.rank(way) > 0)
            def _():
                made.wait_recv()
                total[...] += wide(self.landed[side, last - 1])


def inverse_of(stream):
    return lax.rsqrt(jnp.mean(stream * stream, axis=-1, keepdims=True) + EPS)


def set_shard(values, shard, pieces):
    rounded = low(values)
    shard[...] = rounded
    block = pieces.shape[-1]
    for number in range(pieces.shape[0]):
        pieces[number] = rounded[:, number * block : (number + 1) * block]


def joined(total, exchanged):
    block = exchanged.shape[-1]
    return jnp.concatenate(
        [
            total[:, number * block : (number + 1) * block] + wide(exchanged[number])
            for number in range(exchanged.shape[0])
        ],
        axis=-1,
    )


def turn(values, cosine, sine, direction):
    other = pltpu.roll(values, HD // 2, 1)
    if direction > 0:
        return values * cosine + other * sine
    return values * cosine - other * sine


def head(index):
    return slice(index * HD, (index + 1) * HD)


def allowed_keys(length):
    row_index = lax.broadcasted_iota(jnp.int32, (LEN, LEN), 0)
    column_index = lax.broadcasted_iota(jnp.int32, (LEN, LEN), 1)
    return (column_index <= row_index) & (column_index < length)


def softmax_weights(queries, keys, allowed):
    powers = jnp.where(allowed, jnp.exp(contract_last(queries, keys) * SCALE), 0.0)
    return powers / jnp.sum(powers, axis=-1, keepdims=True)


def centred(weights, values):
    return weights * (values - jnp.sum(weights * values, axis=-1, keepdims=True))


def each_head(total_rows, query_width, key_width):
    repeat = query_width // key_width
    for seq in range(total_rows // LEN):
        rows = slice(seq * LEN, (seq + 1) * LEN)
        for number in range(key_width // HD):
            yield seq, rows, number, range(number * repeat, (number + 1) * repeat)


def repeated(count, function):
    def once(index, carry):
        function(index)
        return carry

    lax.fori_loop(0, count, once, 0)


def columns(index, size):
    return pl.ds(pl.multiple_of(index * size, size), size)


def rows_of(block):
    return block.reshape(-1, block.shape[-1])


def project(source, weights, layer, acc, cut):
    acc[...] = jnp.zeros_like(acc)
    widths = [weight.shape[-1] for weight in weights]

    def once(index):
        at = columns(index, cut)
        part = rows_of(source[:, :, at])
        start = 0
        for weight, width in zip(weights, widths):
            acc[:, start : start + width] += matmul(part, weight[layer, at, :])
            start += width

    repeated(source.shape[-1] // cut, once)


def probe_terms(blocks, probes, layer, partial):
    def once(index):
        rows = rows_of(blocks[index])
        start = 0
        for probe in probes:
            width = probe.shape[-1]
            partial[index, :, start : start + width] = low(matmul(rows, probe[layer]))
            start += width

    repeated(blocks.shape[0], once)


def out_terms(mixed, weight, layer, terms, cut):
    def once(index):
        at = columns(index, cut)
        terms[:, :, at] = low(matmul(mixed[...], weight[layer, :, at])).reshape(
            terms.shape[0], terms.shape[1], cut
        )

    repeated(terms.shape[-1] // cut, once)


def out_probe_terms(blended_all, probe, layer, probed):
    def once(index):
        probed[index] = low(matmul(blended_all[index], probe[layer])).reshape(probed.shape[1:])

    repeated(probed.shape[0], once)


def primal_attention(lengths, acc, cosine, sine, queries, keys, values, blended):
    total_rows, query_width = queries.shape
    key_width = keys.shape[1]
    values[...] = low(acc[:, query_width + key_width :])
    for seq, rows, number, members in each_head(total_rows, query_width, key_width):
        allowed = allowed_keys(lengths[seq])
        key_at = head(query_width // HD + number)
        key_head = low(turn(acc[rows, key_at], cosine[...], sine[...], 1))
        keys[rows, head(number)] = key_head
        value_head = values[rows, head(number)]
        for member in members:
            query_head = low(turn(acc[rows, head(member)], cosine[...], sine[...], 1))
            queries[rows, head(member)] = query_head
            weights = low(softmax_weights(query_head, key_head, allowed))
            blended[rows, head(member)] = low(matmul(weights, value_head))


def tangent_attention(lengths, acc, cosine, sine, queries, keys, values, mixed):
    query_width, key_width = queries.shape[1], keys.shape[1]
    for seq, rows, number, members in each_head(queries.shape[0], query_width, key_width):
        allowed = allowed_keys(lengths[seq])
        key_head = keys[rows, head(number)]
        value_head = values[rows, head(number)]
        key_at = query_width // HD + number
        value_at = key_at + key_width // HD
        moved_key = low(turn(acc[rows, head(key_at)], cosine[...], sine[...], 1))
        moved_value = low(acc[rows, head(value_at)])
        for member in members:
            query_head = queries[rows, head(member)]
            moved_query = low(turn(acc[rows, head(member)], cosine[...], sine[...], 1))
            weights = softmax_weights(query_head, key_head, allowed)
            scores = SCALE * (
                contract_last(moved_query, key_head) + contract_last(query_head, moved_key)
            )
            moved_weights = low(centred(weights, scores))
            mixed[rows, head(member)] = low(
                matmul(moved_weights, value_head) + matmul(low(weights), moved_value)
            )


def mixed_grads(cotangent, weight, layer, acc, cut):
    query_width = weight.shape[1]
    acc[:, :query_width] = jnp.zeros((acc.shape[0], query_width), jnp.float32)

    def once(index):
        at = columns(index, cut)
        acc[:, :query_width] += contract_last(rows_of(cotangent[:, :, at]), weight[layer, :, at])

    repeated(cotangent.shape[-1] // cut, once)


def backward_attention(lengths, acc, cosine, sine, queries, keys, values, grads):
    query_width, key_width = queries.shape[1], keys.shape[1]
    for seq, rows, number, members in each_head(queries.shape[0], query_width, key_width):
        allowed = allowed_keys(lengths[seq])
        key_head = keys[rows, head(number)]
        value_head = values[rows, head(number)]
        key_at = query_width // HD + number
        value_at = key_at + key_width // HD
        key_total = jnp.zeros((LEN, HD), jnp.float32)
        value_total = jnp.zeros((LEN, HD), jnp.float32)
        for member in members:
            query_head = queries[rows, head(member)]
            mixed = low(acc[rows, head(member)])
            weights = softmax_weights(query_head, key_head, allowed)
            value_total = value_total + contract_rows(low(weights), mixed)
            scores = low(centred(weights, contract_last(mixed, value_head)) * SCALE)
            grads[rows, head(member)] = low(
                turn(matmul(scores, key_head), cosine[...], sine[...], -1)
            )
            key_total = key_total + contract_rows(scores, query_head)
        grads[rows, head(key_at)] = low(turn(key_total, cosine[...], sine[...], -1))
        grads[rows, head(value_at)] = low(value_total)


def grad_terms(grads, weights, layer, terms, cut):
    def once(index):
        at = columns(index, cut)
        total = 0.0
        start = 0
        for weight in weights:
            width = weight.shape[-1]
            total = total + contract_last(grads[:, start : start + width], weight[layer, at, :])
            start += width
        terms[:, :, at] = low(total).reshape(terms.shape[0], terms.shape[1], cut)

    repeated(terms.shape[-1] // cut, once)


class Loads:
    def __init__(self, pairs, layers, semaphores):
        self.made = {}
        number = 0
        for layer in range(layers):
            for name, source, target in pairs:
                made = pltpu.make_async_copy(
                    source.at[layer], target.at[layer], semaphores.at[number]
                )
                made.start()
                self.made[name, layer] = made
                number += 1

    def need(self, layer, *names):
        for name in names:
            self.made.pop((name, layer)).wait()


PROJECTIONS = ("query_weight", "key_weight", "value_weight")
PROBES = ("query_probe", "key_probe", "value_probe")


def flow_kernel(sizes, cut, names, *refs):
    m = types.SimpleNamespace(**dict(zip(names, refs)))
    fabric = Fabric(sizes, m.send, m.recv)
    ready = fabric.greet()
    loaded = PROJECTIONS + ("out_weight",) + PROBES + ("out_probe",)
    loads = Loads(
        [(name, getattr(m, name), getattr(m, name + "_held")) for name in loaded],
        m.query_weight.shape[0],
        m.load_sem,
    )
    weights = [getattr(m, name + "_held") for name in PROJECTIONS]
    probes = [getattr(m, name + "_held") for name in PROBES]
    tables = (m.cosine, m.sine)
    kept = [(m.queries.at[layer], m.keys.at[layer], m.values.at[layer]) for layer in range(2)]
    blended = [m.blended.at[layer] for layer in range(2)]
    blended_all = [m.blended_all.at[layer] for layer in range(2)]
    partial = [m.partial.at[layer] for layer in range(2)]
    grads = [m.grads.at[layer] for layer in range(2)]
    grads_held = [m.grads_held.at[layer] for layer in range(2)]
    blocks = [m.blocks.at[layer] for layer in range(2)]
    backs = [ScatterChain(fabric, partial[layer], m.returned.at[layer]) for layer in range(2)]
    fetches = [GatherChain(fabric, blended[layer], blended_all[layer]) for layer in range(2)]
    grad_fetches = [GatherChain(fabric, grads[layer], grads_held[layer]) for layer in range(2)]
    middle = list(range(2, fabric.batches - 1))
    whole = lambda col: m.whole.at[col]
    slot = lambda col: m.terms.at[col]
    slot_p = lambda col: m.probed.at[:, col]
    stores = []

    def store(source, target, number):
        made = pltpu.make_async_copy(source, target, m.store_sem.at[number])
        made.start()
        return made

    def onto_blocks(layer):
        return lambda col: blocks[layer].at[:, col]

    stream = wide(m.tokens[...])
    set_shard(stream * inverse_of(stream) * m.gains[0:1, :], m.shard, m.pieces.at[0])
    ready()
    arrived = fabric.exchange(m.pieces.at[0], m.exchanged.at[0])
    forward, finish = fabric.gather(m.shard, whole)
    arrived()
    forward_blocks, finish_blocks = fabric.gather(m.exchanged.at[0], onto_blocks(0))
    forward()
    finish()
    loads.need(0, *PROJECTIONS)
    project(m.whole, weights, 0, m.acc, cut)
    primal_attention(m.lengths, m.acc, *tables, *kept[0], blended[0])
    fetches[0].step(1)
    forward_blocks()
    loads.need(0, "out_weight")
    out_terms(blended[0], m.out_weight_held, 0, m.terms, cut)
    paired = fabric.pair_up(slot, m.beside)
    finish_blocks()
    stores.append(store(blocks[0], m.blocks0, 0))
    loads.need(0, *PROBES)
    probe_terms(blocks[0], probes, 0, partial[0])
    backs[0].step(1)
    fabric.drain()
    total = fabric.spread(slot, paired, m.beside, m.landed)()

    rounded = low(wide(m.tokens[...]) + total)
    m.stream[...] = rounded
    stream = wide(rounded)
    fabric.drain()
    set_shard(stream * inverse_of(stream) * m.gains[1:2, :], m.shard, m.pieces.at[1])
    arrived = fabric.exchange(m.pieces.at[1], m.exchanged.at[1])
    forward, finish = fabric.gather(m.shard, whole)
    for step in middle:
        backs[0].step(step)
        fetches[0].step(step)
    arrived()
    forward_blocks, finish_blocks = fabric.gather(m.exchanged.at[1], onto_blocks(1))
    forward()
    finish()
    backs[0].step(fabric.batches - 1)
    fetches[0].step(fabric.batches - 1)
    loads.need(1, *PROJECTIONS)
    project(m.whole, weights, 1, m.acc, cut)
    primal_attention(m.lengths, m.acc, *tables, *kept[1], blended[1])
    forward_blocks()
    fetches[0].finish()
    backs[0].finish(m.acc)
    tangent_attention(m.lengths, m.acc, *tables, *kept[0], m.mixed)
    loads.need(0, "out_probe")
    out_probe_terms(blended_all[0], m.out_probe_held, 0, m.probed)
    paired_p = fabric.pair_up(slot_p, m.beside_p)
    out_terms(m.mixed, m.out_weight_held, 0, m.terms, cut)
    paired = fabric.pair_up(slot, m.beside)
    finish_blocks()
    stores.append(store(blocks[1], m.blocks1, 1))
    stores.append(store(blended_all[0], m.blended_all0, 2))
    loads.need(1, *PROBES)
    probe_terms(blocks[1], probes, 1, partial[1])
    backs[1].step(1)
    fetches[1].step(1)

    fabric.drain()
    finish_p = fabric.spread(slot_p, paired_p, m.beside_p, m.landed_p)
    finish = fabric.spread(slot, paired, m.beside, m.landed)
    m.pieces[0] = low(finish_p())
    arrived = fabric.exchange(m.pieces.at[0], m.exchanged.at[2])
    for step in middle:
        backs[1].step(step)
        fetches[1].step(step)
    total = finish()
    arrived()
    change = joined(total, m.exchanged.at[2])
    m.tangent[...] = change
    stream = wide(m.stream[...])
    inverse = inverse_of(stream)
    shift = jnp.mean(stream * change, axis=-1, keepdims=True)
    m.shard[...] = low(
        m.gains[1:2, :] * (change * inverse - stream * inverse * inverse * inverse * shift)
    )
    forward, finish = fabric.gather(m.shard, whole)
    backs[1].step(fabric.batches - 1)
    fetches[1].step(fabric.batches - 1)
    forward()
    finish()
    fabric.drain()
    project(m.whole, weights, 1, m.acc, cut)
    backs[1].finish(m.moved)
    m.acc[...] += m.moved[...]
    tangent_attention(m.lengths, m.acc, *tables, *kept[1], m.mixed)
    fetches[1].finish()
    stores.append(store(blended_all[1], m.blended_all1, 3))
    loads.need(1, "out_probe", "out_weight")
    out_probe_terms(blended_all[1], m.out_probe_held, 1, m.probed)
    paired_p = fabric.pair_up(slot_p, m.beside_p)
    out_terms(m.mixed, m.out_weight_held, 1, m.terms, cut)
    paired = fabric.pair_up(slot, m.beside)

    finish_p = fabric.spread(slot_p, paired_p, m.beside_p, m.landed_p)
    finish = fabric.spread(slot, paired, m.beside, m.landed)
    fabric.drain_chains()
    m.pieces[1] = low(finish_p())
    arrived = fabric.exchange(m.pieces.at[1], m.exchanged.at[3])
    total = finish()
    arrived()
    cotangent = m.mask[...] * (m.tangent[...] + joined(total, m.exchanged.at[3]))
    m.tangent[...] = cotangent
    set_shard(cotangent, m.shard, m.pieces.at[0])
    forward, finish = fabric.gather(m.shard, whole)
    arrived = fabric.exchange(m.pieces.at[0], m.exchanged.at[4])
    forward()
    finish()
    fabric.drain()
    for made in stores:
        made.wait()
    mixed_grads(m.whole, m.out_weight_held, 1, m.acc, cut)
    backward_attention(m.lengths, m.acc, *tables, *kept[1], grads[1])
    grad_fetches[1].step(1)
    grad_terms(grads[1], weights, 1, m.terms, cut)
    paired = fabric.pair_up(slot, m.beside)

    total = fabric.spread(slot, paired, m.beside, m.landed)()
    stream = wide(m.stream[...])
    inverse = inverse_of(stream)
    scaled = total * m.gains[1:2, :]
    shift = jnp.mean(stream * scaled, axis=-1, keepdims=True)
    cotangent = m.tangent[...] + inverse * (scaled - stream * inverse * inverse * shift)
    fabric.drain()
    set_shard(cotangent, m.shard, m.pieces.at[1])
    forward, finish = fabric.gather(m.shard, whole)
    last_arrived = fabric.exchange(m.pieces.at[1], m.exchanged.at[5])
    arrived()
    forward_blocks, finish_blocks = fabric.gather(m.exchanged.at[4], onto_blocks(0))
    for step in middle:
        grad_fetches[1].step(step)
    forward()
    finish()
    mixed_grads(m.whole, m.out_weight_held, 0, m.acc, cut)
    backward_attention(m.lengths, m.acc, *tables, *kept[0], grads[0])
    grad_fetches[1].step(fabric.batches - 1)
    grad_fetches[0].step(1)
    last_arrived()
    forward_last, finish_last = fabric.gather(m.exchanged.at[5], onto_blocks(1))
    forward_blocks()
    finish_blocks()
    last_stores = [store(blocks[0], m.cotangents1, 0)]
    for step in middle:
        grad_fetches[0].step(step)
    grad_fetches[1].finish()
    last_stores.append(store(grads_held[1], m.grads_all1, 1))
    forward_last()
    grad_fetches[0].step(fabric.batches - 1)
    finish_last()
    last_stores.append(store(blocks[1], m.cotangents0, 2))
    grad_fetches[0].finish()
    last_stores.append(store(grads_held[0], m.grads_all0, 3))
    for made in last_stores:
        made.wait()
    fabric.drain()
    fabric.drain_chains()


def product_kernel(layers, *refs):
    inputs, (query_out, key_out, value_out, out_out) = refs[:-4], refs[-4:]
    layer = pl.program_id(0)
    query_width, key_width = query_out.shape[-1], key_out.shape[-1]
    for number in range(layers):
        blocks, grads, blended, cotangent = inputs[4 * number : 4 * number + 4]

        @pl.when(layer == number)
        def _():
            product = contract_rows(blocks[...], grads[...])
            query_out[0] = product[:, :query_width]
            key_out[0] = product[:, query_width : query_width + key_width]
            value_out[0] = product[:, query_width + key_width :]
            out_out[0] = contract_rows(blended[...], cotangent[...])


CUTS = 4


def body(
    tokens,
    lengths,
    norm_gains,
    query_weight,
    key_weight,
    value_weight,
    out_weight,
    query_probe,
    key_probe,
    value_probe,
    out_probe,
):
    width = lax.axis_size("tensor")
    batches = lax.axis_size("dp")
    sizes = (batches, width)
    tensor_index = lax.axis_index("tensor")
    data_index = lax.axis_index("dp")
    share, model = tokens.shape
    group = share * width
    seq_count = group // LEN
    layers = query_weight.shape[0]
    assert layers == 2
    half_width = key_weight.shape[2]
    query_width = query_weight.shape[2]
    paired = half_width < HD
    key_width = 2 * half_width if paired else half_width
    sent_width = query_width + 2 * half_width
    block = query_probe.shape[1]
    cosine, sine = rope_tables(LEN, HD)
    group_lengths = lax.dynamic_slice_in_dim(lengths, data_index * seq_count, seq_count)
    position = tensor_index * share + jnp.arange(share)
    row_mask = wide(position % LEN < group_lengths[position // LEN])[:, None]
    lower_half = tensor_index % 2 == 0

    def swapped(value):
        pairs = [(source, source ^ 1) for source in range(width)]
        return lax.ppermute(value, "tensor", pairs)

    def join_halves(own_part):
        other_part = swapped(own_part)
        return jnp.where(
            lower_half,
            jnp.concatenate([own_part, other_part], axis=-1),
            jnp.concatenate([other_part, own_part], axis=-1),
        )

    def split_halves(values):
        first, second = values[:, :half_width], values[:, half_width:]
        own_part = jnp.where(lower_half, first, second)
        other_part = jnp.where(lower_half, second, first)
        return low(wide(own_part) + wide(swapped(other_part)))

    parts = [key_weight, value_weight, key_probe, value_probe]
    if paired:
        parts = [join_halves(part) for part in parts]
    key_full, value_full, key_probe_full, value_probe_full = parts

    def to_send(grads):
        if not paired:
            return grads
        return jnp.concatenate(
            [
                grads[:, :query_width],
                split_halves(grads[:, query_width : query_width + key_width]),
                split_halves(grads[:, query_width + key_width :]),
            ],
            axis=-1,
        )

    bf, f32 = jnp.bfloat16, jnp.float32
    chips = width // 2
    wide_width = query_width + 2 * key_width
    rows_in_all = batches * group

    def flow():
        inputs = dict(
            lengths=group_lengths,
            tokens=tokens,
            gains=norm_gains,
            mask=row_mask,
            cosine=cosine,
            sine=sine,
            query_weight=query_weight,
            key_weight=key_full,
            value_weight=value_full,
            out_weight=out_weight,
            query_probe=query_probe,
            key_probe=key_probe_full,
            value_probe=value_probe_full,
            out_probe=out_probe,
        )
        blocks_shape = (batches, width, share, block)
        outputs = dict(
            blocks0=blocks_shape,
            blocks1=blocks_shape,
            blended_all0=(batches, group, query_width),
            blended_all1=(batches, group, query_width),
            cotangents0=blocks_shape,
            cotangents1=blocks_shape,
            grads_all0=(batches, group, wide_width),
            grads_all1=(batches, group, wide_width),
        )
        held = {
            name + "_held": pltpu.VMEM(value.shape, bf)
            for name, value in list(inputs.items())[6:]
        }
        scratch = dict(
            whole=pltpu.VMEM((width, share, model), bf),
            blocks=pltpu.VMEM((layers,) + blocks_shape, bf),
            terms=pltpu.VMEM((width, share, model), bf),
            probed=pltpu.VMEM(blocks_shape, bf),
            beside=pltpu.VMEM((chips, share, model), bf),
            landed=pltpu.VMEM((chips, share, model), bf),
            beside_p=pltpu.VMEM((chips, batches, share, block), bf),
            landed_p=pltpu.VMEM((chips, batches, share, block), bf),
            partial=pltpu.VMEM((layers, batches, group, wide_width), bf),
            returned=pltpu.VMEM((layers, 2, batches - 1, group, wide_width), bf),
            queries=pltpu.VMEM((layers, group, query_width), bf),
            keys=pltpu.VMEM((layers, group, key_width), bf),
            values=pltpu.VMEM((layers, group, key_width), bf),
            blended=pltpu.VMEM((layers, group, query_width), bf),
            blended_all=pltpu.VMEM((layers, batches, group, query_width), bf),
            mixed=pltpu.VMEM((group, query_width), bf),
            grads=pltpu.VMEM((layers, group, wide_width), bf),
            grads_held=pltpu.VMEM((layers, batches, group, wide_width), bf),
            acc=pltpu.VMEM((group, wide_width), f32),
            moved=pltpu.VMEM((group, wide_width), f32),
            shard=pltpu.VMEM((share, model), bf),
            stream=pltpu.VMEM((share, model), bf),
            tangent=pltpu.VMEM((share, model), f32),
            pieces=pltpu.VMEM((2, batches, share, block), bf),
            exchanged=pltpu.VMEM((6, batches, share, block), bf),
            **held,
            send=pltpu.SemaphoreType.DMA((semaphore_count(sizes),)),
            recv=pltpu.SemaphoreType.DMA((semaphore_count(sizes),)),
            load_sem=pltpu.SemaphoreType.DMA((layers * len(held),)),
            store_sem=pltpu.SemaphoreType.DMA((4,)),
        )
        vmem = pl.BlockSpec(memory_space=pltpu.VMEM)
        anywhere = pl.BlockSpec(memory_space=pl.ANY)
        return pl.pallas_call(
            functools.partial(
                flow_kernel, sizes, model // CUTS, [*inputs, *outputs, *scratch]
            ),
            out_shape=[jax.ShapeDtypeStruct(shape, bf) for shape in outputs.values()],
            in_specs=[pl.BlockSpec(memory_space=pltpu.SMEM)]
            + [vmem] * 5
            + [anywhere] * len(held),
            out_specs=[anywhere] * len(outputs),
            scratch_shapes=list(scratch.values()),
            compiler_params=pltpu.CompilerParams(
                collective_id=0, has_side_effects=True, vmem_limit_bytes=67043328
            ),
        )(*inputs.values())

    def cost(flops, moved_bytes):
        return pl.CostEstimate(flops=flops, bytes_accessed=moved_bytes, transcendentals=0)

    def products(per_layer):
        out_block = out_probe.shape[2]
        by_rows = query_width % (CUTS * HD) == 0
        blended_cut = query_width // CUTS if by_rows else query_width
        out_cut = out_block if by_rows else out_block // CUTS
        in_specs, args = [], []
        for number, (blocks, grads, blended, cotangents) in enumerate(per_layer):

            def place(i, j, number=number):
                return (0, jnp.clip((i - number) * CUTS + j, 0, CUTS - 1))

            def still(i, j):
                return (0, 0)

            in_specs += [
                pl.BlockSpec((rows_in_all, block // CUTS), place),
                pl.BlockSpec((rows_in_all, sent_width), still),
                pl.BlockSpec((rows_in_all, blended_cut), place if by_rows else still),
                pl.BlockSpec((rows_in_all, out_cut), still if by_rows else place),
            ]
            args += [
                blocks.reshape(rows_in_all, block),
                grads.reshape(rows_in_all, sent_width),
                blended.reshape(rows_in_all, query_width),
                cotangents.reshape(rows_in_all, out_block),
            ]
        shapes = [
            (block, query_width),
            (block, half_width),
            (block, half_width),
            (query_width, out_block),
        ]
        return pl.pallas_call(
            functools.partial(product_kernel, layers),
            grid=(layers, CUTS),
            in_specs=in_specs,
            out_specs=[
                pl.BlockSpec((1, rows // CUTS, columns), lambda i, j: (i, j, 0))
                for rows, columns in shapes[:3]
            ]
            + [
                pl.BlockSpec(
                    (1, blended_cut, out_cut),
                    lambda i, j: (i, j, 0) if by_rows else (i, 0, j),
                )
            ],
            out_shape=[
                jax.ShapeDtypeStruct((layers, rows, columns), f32) for rows, columns in shapes
            ],
            compiler_params=pltpu.CompilerParams(
                dimension_semantics=("arbitrary", "arbitrary")
            ),
            cost_estimate=cost(2 * rows_in_all * block * query_width * 4, 32 << 20),
        )(*args)

    results = flow()
    blocks0, blocks1, blended0, blended1, cotangents0, cotangents1, grads0, grads1 = results
    sent = [to_send(grads.reshape(rows_in_all, wide_width)) for grads in (grads0, grads1)]
    return tuple(
        products(
            [
                (blocks0, sent[0], blended0, cotangents0),
                (blocks1, sent[1], blended1, cotangents1),
            ]
        )
    )


def solution(mesh):
    placed = (
        P(("dp", "tensor"), None),
        P(),
        P(),
        P(None, None, "tensor"),
        P(None, None, "tensor"),
        P(None, None, "tensor"),
        P(None, "tensor", None),
        P(None, "dp", "tensor"),
        P(None, "dp", "tensor"),
        P(None, "dp", "tensor"),
        P(None, "tensor", "dp"),
    )
    return jax.shard_map(
        body,
        mesh=mesh,
        in_specs=placed,
        out_specs=(
            P(None, "dp", "tensor"),
            P(None, "dp", "tensor"),
            P(None, "dp", "tensor"),
            P(None, "tensor", "dp"),
        ),
        check_vma=False,
    )
```

profile of v0, /device:TPU:0, one launch (start us, length us, event | category | flops | bytes accessed | tf_op | source)
XLA Modules:
  0.0 277.2 jit_solution(3160925462403374494)
XLA Ops:
  0.6 1.2 dynamic_slice.5.refs_0_
  1.9 1.3 fusion.5.refs_3_
  3.2 0.5 fusion
  3.7 0.8 pad_maximum_fusion
  4.5 258.4 %shard_map.138 = (bf16[4,8,32,1024]{3,2,1,0:T(8,128)(2,1)}, bf16[4,8,32,1024]{3,2,1,0:T(8,128)(2,1)}, bf16[4,256,512]{2,1,0:T(8,128)(2,1)}, bf16[4,256,512]{2,1,...) custom-call(s32[1]{0:T(128)} %dynamic_slice.5.refs_0_, ...), custom_call_target="tpu_custom_call" | custom-call | tf_op jit(solution)/shard_map/pallas_call | solution.py:884
  262.9 14.2 %shard_map.139 = (f32[2,1024,512]{2,1,0:T(8,128)}, f32[2,1024,128]{2,1,0:T(8,128)}, f32[2,1024,128]{2,1,0:T(8,128)}, f32[2,512,1024]{2,1,0:T(8,128)}) custom-call(bf16[1024,1024]{1,0:T(8,128)(2,1)} %bitcast.9, bf16[1024,768]{1,0:T(8,128)(2,1)} %bitcast.13, bf16[1024,512]{1,0:T(8,128)(2,1)} %bitcast.15, bf16[1024,1024]{1,0:T(8,128)(2,1)} %bitcast.11, ...), custom_call_target="tpu_custom_call" | custom-call | flops 4294967296 | bytes 33554432 | tf_op jit(solution)/shard_map/pallas_call | solution.py:934
  (2 shorter events, 0.0 us)
where the time goes:
time: 278 us; the launch traced here: 277 us
  Pallas kernels  273 us (98%)
    pallas_call x1, Pallas kernels, flow(): pl.pallas_call(functools.partial(flow_kernel, sizes, model // CUTS, [*inp...  258 us
    pallas_call x1, Pallas kernels, products(): pl.pallas_call(functools.partial(product_kernel, layers), grid=(layers, C...  14.2 us

commit v1 on v0

--- a/solution.py
+++ b/solution.py
@@ -4,6 +4,7 @@
 
 import jax
 import jax.numpy as jnp
+import numpy as np
 from jax import lax
 from jax.experimental import pallas as pl
 from jax.experimental.pallas import tpu as pltpu
@@ -42,14 +43,12 @@
 
 
 def rope_tables(length, head_size):
-    position = jnp.arange(length).astype(jnp.float32)
-    column = jnp.arange(head_size // 2).astype(jnp.float32)
-    frequency = jnp.exp(-math.log(THETA) * 2.0 * column / head_size)
-    angles = position[:, None] * frequency[None, :]
-    cosine, sine = jnp.cos(angles), jnp.sin(angles)
+    frequency = np.exp(-math.log(THETA) * 2.0 * np.arange(head_size // 2) / head_size)
+    angles = np.arange(length)[:, None] * frequency.astype(np.float32)[None, :]
+    cosine, sine = np.cos(angles), np.sin(angles)
     return (
-        jnp.concatenate([cosine, cosine], axis=-1),
-        jnp.concatenate([-sine, sine], axis=-1),
+        np.concatenate([cosine, cosine], axis=-1).astype(np.float32),
+        np.concatenate([-sine, sine], axis=-1).astype(np.float32),
     )
 
 
@@ -65,7 +64,7 @@
 
 def semaphore_count(sizes):
     batches, width = sizes
-    return 14 * width + 18 * batches
+    return 24 * width + 18 * batches
 
 
 class Fabric:
@@ -94,10 +93,11 @@
         self.pending.append(made)
         return made
 
-    def drain(self):
-        for made in self.pending:
+    def drain(self, only=None):
+        for made in self.pending if only is None else only:
             made.wait_send()
-        self.pending = []
+        gone = set() if only is None else {id(made) for made in only}
+        self.pending = [made for made in self.pending if gone and id(made) not in gone]
 
     def drain_chains(self):
         for condition, made in self.guarded:
@@ -123,58 +123,6 @@
             pl.semaphore_signal(barrier, inc=1, device_id=peer, device_id_type=MESH)
         return lambda: pl.semaphore_wait(barrier, len(peers))
 
-    def gather(self, source, slot):
-        there = slot(self.col)
-        direct = [
-            self.copy(source, there, self.row, self.peer(step)) for step in range(1, self.chips)
-        ]
-        beside = [self.copy(source, there, self.row, self.mate())]
-        there[...] = source[...]
-
-        def forward():
-            for step in range(1, self.chips):
-                direct[step - 1].wait_recv()
-                piece = slot(self.peer(step))
-                beside.append(self.copy(piece, piece, self.row, self.mate()))
-
-        def finish():
-            for made in beside:
-                made.wait_recv()
-
-        return forward, finish
-
-    def pair_up(self, slot, beside):
-        return [
-            self.copy(slot(flip(self.mate(), 2 * step)), beside.at[step], self.row, self.mate())
-            for step in range(self.chips)
-        ]
-
-    def spread(self, slot, copies, beside, landed):
-        def send(step):
-            return self.copy(slot(self.peer(step)), landed.at[step], self.row, self.peer(step))
-
-        sent = []
-        order = list(range(self.chips - 1, 0, -1))
-        for place, step in enumerate(order):
-            copies[step].wait_recv()
-            own = slot(self.peer(step))
-            own[...] = low(wide(own[...]) + wide(beside[step]))
-            if place:
-                sent.append(send(order[place - 1]))
-        copies[0].wait_recv()
-        total = wide(slot(self.col)[...]) + wide(beside[0])
-        if order:
-            sent.append(send(order[-1]))
-
-        def finish():
-            result = total
-            for made, step in zip(sent, order):
-                made.wait_recv()
-                result = result + wide(landed[step])
-            return result
-
-        return finish
-
     def exchange(self, source, target):
         made = [
             self.copy(
@@ -208,6 +156,142 @@
 
     def rank(self, way):
         return self.row if way > 0 else self.batches - 1 - self.row
+
+
+class Gather:
+    def __init__(self, fabric, source, slot, half):
+        self.fabric, self.slot, self.half = fabric, slot, half
+        self.made, self.beside = [], []
+        there = slot(fabric.col)
+        if fabric.chips == 4:
+            self.first = [
+                self.copy(half(source, 0), half(there, 0), fabric.peer(1)),
+                self.copy(half(source, 1), half(there, 1), fabric.peer(2)),
+            ]
+            self.second = [
+                self.copy(half(source, 1), half(there, 1), fabric.peer(1)),
+                self.copy(half(source, 0), half(there, 0), fabric.peer(2)),
+            ]
+        else:
+            self.direct = [
+                self.copy(source, there, fabric.peer(step)) for step in range(1, fabric.chips)
+            ]
+        self.beside.append(self.copy(source, there, fabric.mate()))
+        there[...] = source[...]
+
+    def copy(self, source, target, col):
+        made = self.fabric.copy(source, target, self.fabric.row, col)
+        self.made.append(made)
+        return made
+
+    def beside_too(self, piece):
+        self.beside.append(self.copy(piece, piece, self.fabric.mate()))
+
+    def relay(self):
+        fabric = self.fabric
+        self.relayed = []
+        if fabric.chips == 4:
+            for number in range(2):
+                self.first[number].wait_recv()
+                piece = self.half(self.slot(fabric.peer(1 + number)), number)
+                self.relayed.append(self.copy(piece, piece, fabric.peer(2 - number)))
+                self.beside_too(piece)
+
+    def forward(self):
+        fabric = self.fabric
+        if fabric.chips == 4:
+            for number in range(2):
+                self.second[number].wait_recv()
+                self.beside_too(self.half(self.slot(fabric.peer(1 + number)), 1 - number))
+            for number in range(2):
+                self.relayed[number].wait_recv()
+                self.beside_too(self.half(self.slot(fabric.peer(3)), number))
+        else:
+            for step in range(1, fabric.chips):
+                self.direct[step - 1].wait_recv()
+                self.beside_too(self.slot(fabric.peer(step)))
+
+    def finish(self):
+        for made in self.beside:
+            made.wait_recv()
+
+    def drain(self):
+        self.fabric.drain(self.made)
+
+
+class Reduce:
+    def __init__(self, fabric, slot, beside, landed, relayed, half):
+        self.fabric, self.slot, self.half = fabric, slot, half
+        self.beside, self.landed, self.relayed = beside, landed, relayed
+        self.paired = [
+            fabric.copy(
+                slot(flip(fabric.mate(), 2 * step)), beside.at[step], fabric.row, fabric.mate()
+            )
+            for step in range(fabric.chips)
+        ]
+
+    def add(self, step):
+        self.paired[step].wait_recv()
+        own = self.slot(self.fabric.peer(step))
+        own[...] = low(wide(own[...]) + wide(self.beside[step]))
+
+    def part(self, step, number):
+        return self.half(self.slot(self.fabric.peer(step)), number)
+
+    def send(self, step, number=None):
+        fabric = self.fabric
+        if number is None:
+            source, target = self.slot(fabric.peer(step)), self.landed.at[step]
+        else:
+            source, target = self.part(step, number), self.half(self.landed.at[step], number)
+        self.sent.append((step, number, fabric.copy(source, target, fabric.row, fabric.peer(step))))
+
+    def spread(self):
+        fabric = self.fabric
+        self.sent = []
+        if fabric.chips == 4:
+            self.add(3)
+            self.add(1)
+            self.passed = [
+                fabric.copy(
+                    self.part(3, number),
+                    self.relayed.at[number],
+                    fabric.row,
+                    fabric.peer(1 + number),
+                )
+                for number in range(2)
+            ]
+            self.add(2)
+            self.send(1, 0)
+        else:
+            order = list(range(fabric.chips - 1, 0, -1))
+            for place, step in enumerate(order):
+                self.add(step)
+                if place:
+                    self.send(order[place - 1])
+        self.paired[0].wait_recv()
+        self.total = wide(self.slot(fabric.col)[...]) + wide(self.beside[0])
+        if fabric.chips == 4:
+            self.send(2, 1)
+        elif order:
+            self.send(order[-1])
+
+    def relay(self):
+        if self.fabric.chips == 4:
+            for number in range(2):
+                self.passed[number].wait_recv()
+                part = self.part(2 - number, number)
+                part[...] = low(wide(part[...]) + wide(self.relayed[number]))
+                self.send(2 - number, number)
+
+    def finish(self):
+        result = self.total
+        for step, number, made in self.sent:
+            made.wait_recv()
+        for step in range(1, self.fabric.chips):
+            if self.fabric.chips != 4 or step < 3:
+                result = result + wide(self.landed[step])
+        return result
 
 
 class GatherChain:
@@ -546,90 +630,132 @@
     backs = [ScatterChain(fabric, partial[layer], m.returned.at[layer]) for layer in range(2)]
     fetches = [GatherChain(fabric, blended[layer], blended_all[layer]) for layer in range(2)]
     grad_fetches = [GatherChain(fabric, grads[layer], grads_held[layer]) for layer in range(2)]
+    share, model = m.tokens.shape
+    sequences = m.whole.shape[0] * share // LEN
+    lengths = [m.lengths[fabric.row * sequences + number] for number in range(sequences)]
     middle = list(range(2, fabric.batches - 1))
-    whole = lambda col: m.whole.at[col]
-    slot = lambda col: m.terms.at[col]
-    slot_p = lambda col: m.probed.at[:, col]
+    final = fabric.batches - 1
     stores = []
+
+    def whole(col):
+        return m.whole.at[col]
+
+    def slot(col):
+        return m.terms.at[col]
+
+    def slot_p(col):
+        return m.probed.at[:, col]
+
+    def onto_blocks(layer):
+        return lambda col: blocks[layer].at[:, col]
+
+    def half(ref, number):
+        return ref.at[:, number * (model // 2) : (number + 1) * (model // 2)]
+
+    def half_p(ref, number):
+        count = fabric.batches // 2
+        return ref.at[number * count : (number + 1) * count]
 
     def store(source, target, number):
         made = pltpu.make_async_copy(source, target, m.store_sem.at[number])
         made.start()
         return made
 
-    def onto_blocks(layer):
-        return lambda col: blocks[layer].at[:, col]
+    def gather_shard():
+        return Gather(fabric, m.shard, whole, half)
+
+    def gather_blocks(number, layer):
+        return Gather(fabric, m.exchanged.at[number], onto_blocks(layer), half_p)
+
+    def exchange(number, place):
+        return fabric.exchange(m.pieces.at[place], m.exchanged.at[number])
+
+    def reduce_terms():
+        return Reduce(fabric, slot, m.beside, m.landed, m.relayed, half)
+
+    def reduce_probed():
+        return Reduce(fabric, slot_p, m.beside_p, m.landed_p, m.relayed_p, half_p)
+
+    def steps(chain, numbers):
+        for number in numbers:
+            chain.step(number)
 
     stream = wide(m.tokens[...])
     set_shard(stream * inverse_of(stream) * m.gains[0:1, :], m.shard, m.pieces.at[0])
     ready()
-    arrived = fabric.exchange(m.pieces.at[0], m.exchanged.at[0])
-    forward, finish = fabric.gather(m.shard, whole)
+    arrived = exchange(0, 0)
+    gathered = gather_shard()
+    gathered.relay()
     arrived()
-    forward_blocks, finish_blocks = fabric.gather(m.exchanged.at[0], onto_blocks(0))
-    forward()
-    finish()
+    gathered_blocks = gather_blocks(0, 0)
+    gathered.forward()
+    gathered.finish()
     loads.need(0, *PROJECTIONS)
     project(m.whole, weights, 0, m.acc, cut)
-    primal_attention(m.lengths, m.acc, *tables, *kept[0], blended[0])
+    gathered_blocks.relay()
+    primal_attention(lengths, m.acc, *tables, *kept[0], blended[0])
     fetches[0].step(1)
-    forward_blocks()
     loads.need(0, "out_weight")
     out_terms(blended[0], m.out_weight_held, 0, m.terms, cut)
-    paired = fabric.pair_up(slot, m.beside)
-    finish_blocks()
+    gathered.drain()
+    summing = reduce_terms()
+    gathered_blocks.forward()
+    summing.spread()
+    gathered_blocks.finish()
     stores.append(store(blocks[0], m.blocks0, 0))
     loads.need(0, *PROBES)
     probe_terms(blocks[0], probes, 0, partial[0])
     backs[0].step(1)
-    fabric.drain()
-    total = fabric.spread(slot, paired, m.beside, m.landed)()
+    summing.relay()
+    total = summing.finish()
 
     rounded = low(wide(m.tokens[...]) + total)
     m.stream[...] = rounded
     stream = wide(rounded)
-    fabric.drain()
     set_shard(stream * inverse_of(stream) * m.gains[1:2, :], m.shard, m.pieces.at[1])
-    arrived = fabric.exchange(m.pieces.at[1], m.exchanged.at[1])
-    forward, finish = fabric.gather(m.shard, whole)
-    for step in middle:
-        backs[0].step(step)
-        fetches[0].step(step)
+    arrived = exchange(1, 1)
+    gathered = gather_shard()
+    gathered.relay()
+    steps(backs[0], middle)
+    steps(fetches[0], middle)
     arrived()
-    forward_blocks, finish_blocks = fabric.gather(m.exchanged.at[1], onto_blocks(1))
-    forward()
-    finish()
-    backs[0].step(fabric.batches - 1)
-    fetches[0].step(fabric.batches - 1)
+    gathered_blocks = gather_blocks(1, 1)
+    gathered.forward()
+    gathered.finish()
     loads.need(1, *PROJECTIONS)
     project(m.whole, weights, 1, m.acc, cut)
-    primal_attention(m.lengths, m.acc, *tables, *kept[1], blended[1])
-    forward_blocks()
+    gathered_blocks.relay()
+    backs[0].step(final)
+    primal_attention(lengths, m.acc, *tables, *kept[1], blended[1])
+    fetches[0].step(final)
+    gathered_blocks.forward()
+    gathered_blocks.finish()
+    stores.append(store(blocks[1], m.blocks1, 1))
+    loads.need(1, *PROBES)
+    probe_terms(blocks[1], probes, 1, partial[1])
+    backs[0].finish(m.acc)
+    backs[1].step(1)
+    fetches[1].step(1)
+    tangent_attention(lengths, m.acc, *tables, *kept[0], m.mixed)
     fetches[0].finish()
-    backs[0].finish(m.acc)
-    tangent_attention(m.lengths, m.acc, *tables, *kept[0], m.mixed)
+    stores.append(store(blended_all[0], m.blended_all0, 2))
+    fabric.drain()
     loads.need(0, "out_probe")
     out_probe_terms(blended_all[0], m.out_probe_held, 0, m.probed)
-    paired_p = fabric.pair_up(slot_p, m.beside_p)
+    summing_p = reduce_probed()
     out_terms(m.mixed, m.out_weight_held, 0, m.terms, cut)
-    paired = fabric.pair_up(slot, m.beside)
-    finish_blocks()
-    stores.append(store(blocks[1], m.blocks1, 1))
-    stores.append(store(blended_all[0], m.blended_all0, 2))
-    loads.need(1, *PROBES)
-    probe_terms(blocks[1], probes, 1, partial[1])
-    backs[1].step(1)
-    fetches[1].step(1)
-
-    fabric.drain()
-    finish_p = fabric.spread(slot_p, paired_p, m.beside_p, m.landed_p)
-    finish = fabric.spread(slot, paired, m.beside, m.landed)
-    m.pieces[0] = low(finish_p())
-    arrived = fabric.exchange(m.pieces.at[0], m.exchanged.at[2])
-    for step in middle:
-        backs[1].step(step)
-        fetches[1].step(step)
-    total = finish()
+    summing = reduce_terms()
+
+    summing_p.spread()
+    summing_p.relay()
+    summing.spread()
+    steps(backs[1], middle)
+    summing.relay()
+    m.pieces[0] = low(summing_p.finish())
+    arrived = exchange(2, 0)
+    steps(fetches[1], middle)
+    backs[1].step(final)
+    total = summing.finish()
     arrived()
     change = joined(total, m.exchanged.at[2])
     m.tangent[...] = change
@@ -639,80 +765,91 @@
     m.shard[...] = low(
         m.gains[1:2, :] * (change * inverse - stream * inverse * inverse * inverse * shift)
     )
-    forward, finish = fabric.gather(m.shard, whole)
-    backs[1].step(fabric.batches - 1)
-    fetches[1].step(fabric.batches - 1)
-    forward()
-    finish()
+    gathered = gather_shard()
+    gathered.relay()
+    fetches[1].step(final)
+    gathered.forward()
+    gathered.finish()
     fabric.drain()
     project(m.whole, weights, 1, m.acc, cut)
     backs[1].finish(m.moved)
     m.acc[...] += m.moved[...]
-    tangent_attention(m.lengths, m.acc, *tables, *kept[1], m.mixed)
+    tangent_attention(lengths, m.acc, *tables, *kept[1], m.mixed)
     fetches[1].finish()
     stores.append(store(blended_all[1], m.blended_all1, 3))
     loads.need(1, "out_probe", "out_weight")
     out_probe_terms(blended_all[1], m.out_probe_held, 1, m.probed)
-    paired_p = fabric.pair_up(slot_p, m.beside_p)
+    summing_p = reduce_probed()
     out_terms(m.mixed, m.out_weight_held, 1, m.terms, cut)
-    paired = fabric.pair_up(slot, m.beside)
-
-    finish_p = fabric.spread(slot_p, paired_p, m.beside_p, m.landed_p)
-    finish = fabric.spread(slot, paired, m.beside, m.landed)
+    summing = reduce_terms()
+
+    summing_p.spread()
+    summing_p.relay()
+    summing.spread()
+    summing.relay()
     fabric.drain_chains()
-    m.pieces[1] = low(finish_p())
-    arrived = fabric.exchange(m.pieces.at[1], m.exchanged.at[3])
-    total = finish()
+    m.pieces[1] = low(summing_p.finish())
+    arrived = exchange(3, 1)
+    total = summing.finish()
     arrived()
-    cotangent = m.mask[...] * (m.tangent[...] + joined(total, m.exchanged.at[3]))
+    first_row = fabric.col * share
+    sequence = lax.div(first_row, LEN)
+    position = first_row - sequence * LEN + lax.broadcasted_iota(jnp.int32, (share, 1), 0)
+    valid = position < m.lengths[fabric.row * sequences + sequence]
+    cotangent = jnp.where(valid, 1.0, 0.0) * (
+        m.tangent[...] + joined(total, m.exchanged.at[3])
+    )
     m.tangent[...] = cotangent
     set_shard(cotangent, m.shard, m.pieces.at[0])
-    forward, finish = fabric.gather(m.shard, whole)
-    arrived = fabric.exchange(m.pieces.at[0], m.exchanged.at[4])
-    forward()
-    finish()
+    gathered = gather_shard()
+    arrived = exchange(4, 0)
+    gathered.relay()
+    gathered.forward()
+    gathered.finish()
     fabric.drain()
     for made in stores:
         made.wait()
     mixed_grads(m.whole, m.out_weight_held, 1, m.acc, cut)
-    backward_attention(m.lengths, m.acc, *tables, *kept[1], grads[1])
+    backward_attention(lengths, m.acc, *tables, *kept[1], grads[1])
     grad_fetches[1].step(1)
     grad_terms(grads[1], weights, 1, m.terms, cut)
-    paired = fabric.pair_up(slot, m.beside)
-
-    total = fabric.spread(slot, paired, m.beside, m.landed)()
+    summing = reduce_terms()
+
+    summing.spread()
+    summing.relay()
+    steps(grad_fetches[1], middle)
+    total = summing.finish()
     stream = wide(m.stream[...])
     inverse = inverse_of(stream)
     scaled = total * m.gains[1:2, :]
     shift = jnp.mean(stream * scaled, axis=-1, keepdims=True)
     cotangent = m.tangent[...] + inverse * (scaled - stream * inverse * inverse * shift)
-    fabric.drain()
     set_shard(cotangent, m.shard, m.pieces.at[1])
-    forward, finish = fabric.gather(m.shard, whole)
-    last_arrived = fabric.exchange(m.pieces.at[1], m.exchanged.at[5])
+    gathered = gather_shard()
+    last_arrived = exchange(5, 1)
+    gathered.relay()
     arrived()
-    forward_blocks, finish_blocks = fabric.gather(m.exchanged.at[4], onto_blocks(0))
-    for step in middle:
-        grad_fetches[1].step(step)
-    forward()
-    finish()
+    gathered_blocks = gather_blocks(4, 0)
+    grad_fetches[1].step(final)
+    gathered.forward()
+    gathered.finish()
     mixed_grads(m.whole, m.out_weight_held, 0, m.acc, cut)
-    backward_attention(m.lengths, m.acc, *tables, *kept[0], grads[0])
-    grad_fetches[1].step(fabric.batches - 1)
+    gathered_blocks.relay()
+    backward_attention(lengths, m.acc, *tables, *kept[0], grads[0])
     grad_fetches[0].step(1)
     last_arrived()
-    forward_last, finish_last = fabric.gather(m.exchanged.at[5], onto_blocks(1))
-    forward_blocks()
-    finish_blocks()
+    gathered_last = gather_blocks(5, 1)
+    gathered_blocks.forward()
+    gathered_blocks.finish()
     last_stores = [store(blocks[0], m.cotangents1, 0)]
-    for step in middle:
-        grad_fetches[0].step(step)
+    gathered_last.relay()
     grad_fetches[1].finish()
     last_stores.append(store(grads_held[1], m.grads_all1, 1))
-    forward_last()
-    grad_fetches[0].step(fabric.batches - 1)
-    finish_last()
+    steps(grad_fetches[0], middle)
+    gathered_last.forward()
+    gathered_last.finish()
     last_stores.append(store(blocks[1], m.cotangents0, 2))
+    grad_fetches[0].step(final)
     grad_fetches[0].finish()
     last_stores.append(store(grads_held[0], m.grads_all0, 3))
     for made in last_stores:
@@ -757,10 +894,9 @@
     batches = lax.axis_size("dp")
     sizes = (batches, width)
     tensor_index = lax.axis_index("tensor")
-    data_index = lax.axis_index("dp")
     share, model = tokens.shape
     group = share * width
-    seq_count = group // LEN
+    assert LEN % share == 0
     layers = query_weight.shape[0]
     assert layers == 2
     half_width = key_weight.shape[2]
@@ -770,9 +906,6 @@
     sent_width = query_width + 2 * half_width
     block = query_probe.shape[1]
     cosine, sine = rope_tables(LEN, HD)
-    group_lengths = lax.dynamic_slice_in_dim(lengths, data_index * seq_count, seq_count)
-    position = tensor_index * share + jnp.arange(share)
-    row_mask = wide(position % LEN < group_lengths[position // LEN])[:, None]
     lower_half = tensor_index % 2 == 0
 
     def swapped(value):
@@ -817,10 +950,9 @@
 
     def flow():
         inputs = dict(
-            lengths=group_lengths,
+            lengths=lengths,
             tokens=tokens,
             gains=norm_gains,
-            mask=row_mask,
             cosine=cosine,
             sine=sine,
             query_weight=query_weight,
@@ -845,7 +977,7 @@
         )
         held = {
             name + "_held": pltpu.VMEM(value.shape, bf)
-            for name, value in list(inputs.items())[6:]
+            for name, value in list(inputs.items())[5:]
         }
         scratch = dict(
             whole=pltpu.VMEM((width, share, model), bf),
@@ -856,6 +988,8 @@
             landed=pltpu.VMEM((chips, share, model), bf),
             beside_p=pltpu.VMEM((chips, batches, share, block), bf),
             landed_p=pltpu.VMEM((chips, batches, share, block), bf),
+            relayed=pltpu.VMEM((2, share, model // 2), bf),
+            relayed_p=pltpu.VMEM((2, batches // 2, share, block), bf),
             partial=pltpu.VMEM((layers, batches, group, wide_width), bf),
             returned=pltpu.VMEM((layers, 2, batches - 1, group, wide_width), bf),
             queries=pltpu.VMEM((layers, group, query_width), bf),
@@ -887,7 +1021,7 @@
             ),
             out_shape=[jax.ShapeDtypeStruct(shape, bf) for shape in outputs.values()],
             in_specs=[pl.BlockSpec(memory_space=pltpu.SMEM)]
-            + [vmem] * 5
+            + [vmem] * 4
             + [anywhere] * len(held),
             out_specs=[anywhere] * len(outputs),
             scratch_shapes=list(scratch.values()),

time: 278 us -> 235 us (0.85)
  Pallas kernels: 273 us -> 234 us
    pallas_call x1, Pallas kernels: 258 us -> 220 us  [flow(): pl.pallas_call(functools.partial(flow_kernel, sizes, model // CUTS, [*inp...]
where the time goes in v1:
time: 235 us
  Pallas kernels  234 us (100%)
    pallas_call x1, Pallas kernels, flow(): pl.pallas_call(functools.partial(flow_kernel, sizes, model // CUTS, [*inp...  220 us
    pallas_call x1, Pallas kernels, products(): pl.pallas_call(functools.partial(product_kernel, layers), grid=(layers, C...  14.2 us

profile of v1, /device:TPU:0, one launch (start us, length us, event | category | flops | bytes accessed | tf_op | source)
XLA Modules:
  0.0 235.2 jit_solution(13563213463692989782)
XLA Ops:
  0.6 220.2 %shard_map.156 = (bf16[4,8,32,1024]{3,2,1,0:T(8,128)(2,1)}, bf16[4,8,32,1024]{3,2,1,0:T(8,128)(2,1)}, bf16[4,256,512]{2,1,0:T(8,128)(2,1)}, bf16[4,256,512]{2,1,...) custom-call(s32[4]{0:T(128)} %refs_0_.1, ...), custom_call_target="tpu_custom_call" | custom-call | tf_op jit(solution)/shard_map/pallas_call | solution.py:1018
  220.8 14.2 %shard_map.157 = (f32[2,1024,512]{2,1,0:T(8,128)}, f32[2,1024,128]{2,1,0:T(8,128)}, f32[2,1024,128]{2,1,0:T(8,128)}, f32[2,512,1024]{2,1,0:T(8,128)}) custom-call(bf16[1024,1024]{1,0:T(8,128)(2,1)} %bitcast.8, bf16[1024,768]{1,0:T(8,128)(2,1)} %bitcast.12, bf16[1024,512]{1,0:T(8,128)(2,1)} %bitcast.14, bf16[1024,1024]{1,0:T(8,128)(2,1)} %bitcast.10, ...), custom_call_target="tpu_custom_call" | custom-call | flops 4294967296 | bytes 33554432 | tf_op jit(solution)/shard_map/pallas_call | solution.py:1068

commit v2 on v1

--- a/solution.py
+++ b/solution.py
@@ -64,7 +64,7 @@
 
 def semaphore_count(sizes):
     batches, width = sizes
-    return 24 * width + 18 * batches
+    return 24 * width + 22 * batches
 
 
 class Fabric:
@@ -295,8 +295,8 @@
 
 
 class GatherChain:
-    def __init__(self, fabric, source, target):
-        self.fabric, self.source, self.target = fabric, source, target
+    def __init__(self, fabric, source, slot):
+        self.fabric, self.source, self.slot = fabric, source, slot
         self.first = fabric.reserve(2 * (fabric.batches - 1))
 
     def number(self, way, step):
@@ -306,9 +306,8 @@
         fabric = self.fabric
         for way in (1, -1):
             piece = jnp.clip(fabric.row - way * step, 0, fabric.batches - 1)
-            made = fabric.hop(
-                self.target.at[piece], self.target.at[piece], self.number(way, step), way
-            )
+            place = self.slot(piece)
+            made = fabric.hop(place, place, self.number(way, step), way)
             pl.when(fabric.rank(way) >= step)(made.wait_recv)
 
     def step(self, step):
@@ -317,17 +316,39 @@
             self.arrive(step - 1)
         for way in (1, -1):
             piece = jnp.clip(fabric.row - way * (step - 1), 0, fabric.batches - 1)
-            source = self.source if step == 1 else self.target.at[piece]
-            made = fabric.hop(source, self.target.at[piece], self.number(way, step), way)
+            place = self.slot(piece)
+            source = self.source if step == 1 else place
+            made = fabric.hop(source, place, self.number(way, step), way)
             rank = fabric.rank(way)
             condition = (rank >= step - 1) & (rank < fabric.batches - 1)
             pl.when(condition)(made.start)
             fabric.guarded.append((condition, made))
         if step == 1:
-            self.target[fabric.row] = self.source[...]
+            self.slot(fabric.row)[...] = self.source[...]
 
     def finish(self):
         self.arrive(self.fabric.batches - 1)
+
+
+class ChainPair:
+    def __init__(self, fabric, source, target):
+        count = source.shape[0] // 2
+        self.chains = [
+            GatherChain(
+                fabric,
+                source.at[first : first + count],
+                lambda piece, first=first: target.at[piece, first : first + count],
+            )
+            for first in (0, count)
+        ]
+
+    def step(self, step):
+        for chain in self.chains:
+            chain.step(step)
+
+    def finish(self):
+        for chain in self.chains:
+            chain.finish()
 
 
 class ScatterChain:
@@ -628,8 +649,11 @@
     grads_held = [m.grads_held.at[layer] for layer in range(2)]
     blocks = [m.blocks.at[layer] for layer in range(2)]
     backs = [ScatterChain(fabric, partial[layer], m.returned.at[layer]) for layer in range(2)]
-    fetches = [GatherChain(fabric, blended[layer], blended_all[layer]) for layer in range(2)]
-    grad_fetches = [GatherChain(fabric, grads[layer], grads_held[layer]) for layer in range(2)]
+    fetches = [
+        GatherChain(fabric, blended[layer], lambda piece, layer=layer: blended_all[layer].at[piece])
+        for layer in range(2)
+    ]
+    grad_fetches = [ChainPair(fabric, grads[layer], grads_held[layer]) for layer in range(2)]
     share, model = m.tokens.shape
     sequences = m.whole.shape[0] * share // LEN
     lengths = [m.lengths[fabric.row * sequences + number] for number in range(sequences)]
@@ -828,10 +852,10 @@
     gathered = gather_shard()
     last_arrived = exchange(5, 1)
     gathered.relay()
+    grad_fetches[1].step(final)
+    gathered.forward()
     arrived()
     gathered_blocks = gather_blocks(4, 0)
-    grad_fetches[1].step(final)
-    gathered.forward()
     gathered.finish()
     mixed_grads(m.whole, m.out_weight_held, 0, m.acc, cut)
     gathered_blocks.relay()
@@ -874,7 +898,8 @@
             out_out[0] = contract_rows(blended[...], cotangent[...])
 
 
-CUTS = 4
+CUTS = 2
+FLOW_CUTS = 2
 
 
 def body(
@@ -1017,7 +1042,7 @@
         anywhere = pl.BlockSpec(memory_space=pl.ANY)
         return pl.pallas_call(
             functools.partial(
-                flow_kernel, sizes, model // CUTS, [*inputs, *outputs, *scratch]
+                flow_kernel, sizes, model // FLOW_CUTS, [*inputs, *outputs, *scratch]
             ),
             out_shape=[jax.ShapeDtypeStruct(shape, bf) for shape in outputs.values()],
             in_specs=[pl.BlockSpec(memory_space=pltpu.SMEM)]

time: 235 us -> 227 us (0.966)
  Pallas kernels: 234 us -> 227 us
    pallas_call x1, Pallas kernels: 220 us -> 214 us  [flow(): pl.pallas_call(functools.partial(flow_kernel, sizes, model // FLOW_CUTS,...]
where the time goes in v2:
time: 227 us
  Pallas kernels  227 us (100%)
    pallas_call x1, Pallas kernels, flow(): pl.pallas_call(functools.partial(flow_kernel, sizes, model // FLOW_CUTS,...  214 us
    pallas_call x1, Pallas kernels, products(): pl.pallas_call(functools.partial(product_kernel, layers), grid=(layers, C...  12.9 us

profile of v2, /device:TPU:0, one launch (start us, length us, event | category | flops | bytes accessed | tf_op | source)
XLA Modules:
  0.0 227.3 jit_solution(2638083667834350381)
XLA Ops:
  0.6 213.8 %shard_map.156 = (bf16[4,8,32,1024]{3,2,1,0:T(8,128)(2,1)}, bf16[4,8,32,1024]{3,2,1,0:T(8,128)(2,1)}, bf16[4,256,512]{2,1,0:T(8,128)(2,1)}, bf16[4,256,512]{2,1,...) custom-call(s32[4]{0:T(128)} %refs_0_.1, ...), custom_call_target="tpu_custom_call" | custom-call | tf_op jit(solution)/shard_map/pallas_call | solution.py:1043
  214.4 12.9 %shard_map.157 = (f32[2,1024,512]{2,1,0:T(8,128)}, f32[2,1024,128]{2,1,0:T(8,128)}, f32[2,1024,128]{2,1,0:T(8,128)}, f32[2,512,1024]{2,1,0:T(8,128)}) custom-call(bf16[1024,1024]{1,0:T(8,128)(2,1)} %bitcast.8, bf16[1024,768]{1,0:T(8,128)(2,1)} %bitcast.12, bf16[1024,512]{1,0:T(8,128)(2,1)} %bitcast.14, bf16[1024,1024]{1,0:T(8,128)(2,1)} %bitcast.10, ...), custom_call_target="tpu_custom_call" | custom-call | flops 4294967296 | bytes 33554432 | tf_op jit(solution)/shard_map/pallas_call | solution.py:1093
